TPU v7x, 32 devices: a whole 2x2x4 slice. The times are simulated.
32 devices in a mesh: dp: 4 (over z), tensor: 8 (over y, x, core).
Axes of the slice: x: 2, y: 2, z: 4, core: 2. Of those that a mesh axis runs over, the one named last changes fastest.
Arguments:
- activations: bfloat16 [1024, 27648], P('dp', 'tensor'), may hold values from -6 to 6
- left_factor: float32 [216, 216], replicated, may hold values from -2 to 3, as said below
- right_factor: float32 [128, 128], replicated, may hold values from -2 to 3, as said below
- clip_scale: float32 [128, 216], replicated, may hold values from 0.5 to 3
- weight_rows: bfloat16 [27648, 5120], P('tensor'), may hold values from -0.0390625 to 0.0390625
- target: bfloat16 [1024, 5120], P('dp'), may hold values from -6 to 6
Outputs:
- grad_left: float32 [216, 216], replicated
- grad_right: float32 [128, 128], replicated
- grad_input: float32 [1024, 27648], P('dp', 'tensor')
Inputs may be any that keep to these rules, and one draw needn't show every extreme that they name: `left_factor`: the identity plus independent entries of order one over the square root of 216. `right_factor`: the identity plus independent entries of order one over the square root of 128.
All inputs are finite; a program needn't handle non-finite values.
Results may differ from a plain program's by a relative error of at most 0.007.
Values may be sent and summed in bfloat16 or wider, within the bound.
A program may use at most 128 MiB of HBM per device.

v0:
```python
import jax
import jax.numpy as jnp
from jax import lax
from jax.sharding import PartitionSpec as P


def local(activations, left_factor, right_factor, clip_scale, weight_rows, target):
    highest = lax.Precision.HIGHEST
    tok_rows = activations.shape[0]
    width_left = left_factor.shape[0]
    local_right = activations.shape[1] // width_left
    inputs = activations.reshape(tok_rows, local_right, width_left)
    moved = lax.all_to_all(inputs, "tensor", split_axis=0, concat_axis=1, tiled=True)
    mixed = jnp.einsum("tji,ik->tjk", moved.astype(jnp.float32), left_factor, precision=highest)
    rotated = jnp.einsum("jl,tjk->tlk", right_factor, mixed, precision=highest)
    bounded = jnp.tanh(rotated / clip_scale)
    clipped = (clip_scale * bounded).astype(jnp.bfloat16)
    clipped_back = lax.all_to_all(clipped, "tensor", split_axis=1, concat_axis=0, tiled=True)
    partial_out = jnp.dot(
        clipped_back.reshape(tok_rows, -1), weight_rows, preferred_element_type=jnp.float32
    )
    total = lax.psum(partial_out, "tensor")
    out_grad = (total - target.astype(jnp.float32)).astype(jnp.bfloat16)
    clipped_grad = lax.dot_general(
        out_grad, weight_rows, (((1,), (1,)), ((), ())), preferred_element_type=jnp.float32
    )
    clipped_grad = clipped_grad.reshape(tok_rows, local_right, width_left)
    grad_owned = lax.all_to_all(clipped_grad, "tensor", split_axis=0, concat_axis=1, tiled=True)
    rotated_grad = grad_owned * (1.0 - bounded * bounded)
    mixed_grad = jnp.einsum("jl,tlk->tjk", right_factor, rotated_grad, precision=highest)
    right_part = jnp.einsum("tjk,tlk->jl", mixed, rotated_grad, precision=highest)
    grad_back = lax.all_to_all(mixed_grad, "tensor", split_axis=1, concat_axis=0, tiled=True)
    input_grad = jnp.einsum("tjk,ik->tji", grad_back, left_factor, precision=highest).reshape(
        tok_rows, -1
    )
    left_part = jnp.einsum("tji,tjk->ik", inputs.astype(jnp.float32), grad_back, precision=highest)
    left_sum, right_sum = lax.psum((left_part, right_part), ("dp", "tensor"))
    return (left_sum, right_sum, input_grad)


def solution(mesh):
    placed = (P("dp", "tensor"), P(), P(), P(), P("tensor", None), P("dp", None))
    return jax.shard_map(
        local, mesh=mesh, in_specs=placed, out_specs=(P(), P(), P("dp", "tensor")), check_vma=False
    )
```

profile of v0, /device:TPU:8, one launch (start us, length us, event | category | flops | bytes accessed | tf_op | source)
XLA Modules:
  0.0 508.3 jit_solution(451690624203319944)
XLA Ops:
  9.9 3.0 copy.32
  12.9 30.3 %all_to_all.69 = bf16[256,16,216]{2,1,0:T(8,128)(2,1)S(1)} all-to-all(bf16[256,16,216]{2,1,0:T(8,128)(2,1)} %copy.32), channel_id=1, replica_groups=mesh['dp'=4,'tensor'=8] {'tensor'}, dimensions={0} | all-to-all | bytes 3538944 | tf_op jit(solution)/shard_map/all_to_all | solution.py:13
  45.7 4.7 multiply_convert_fusion
  50.4 4.5 copy.36
  54.9 30.1 %all_to_all.70 = bf16[32,128,216]{2,0,1:T(8,128)(2,1)S(1)} all-to-all(bf16[32,128,216]{2,0,1:T(8,128)(2,1)} %copy.36), channel_id=1, replica_groups=mesh['dp'=4,'tensor'=8] {'tensor'}, dimensions={1} | all-to-all | bytes 3538944 | tf_op jit(solution)/shard_map/all_to_all | solution.py:18
  87.6 5.2 %reshape.21 = bf16[256,3456]{1,0:T(8,128)(2,1)} reshape(bf16[8,32,16,216]{3,2,1,0:T(8,128)(2,1)} %copy.38) | data formatting | bytes 3538944 | tf_op jit(solution)/shard_map/reshape | solution.py:20
  92.8 18.0 %fusion.12 = f32[256,5120]{1,0:T(8,128)} fusion(bf16[256,3456]{1,0:T(8,128)(2,1)} %reshape.21, bf16[3456,5120]{1,0:T(8,128)(2,1)} %param.10), kind=kOutput, calls=%fused_computation.18 | convolution fusion | flops 9059696640 | bytes 42401792 | tf_op jit(solution)/shard_map/dot_general | solution.py:19
  110.8 91.8 %all-reduce.4.cloned.1.call-done = f32[256,5120]{1,0:T(8,128)} async-done(((f32[256,5120]{1,0:T(8,128)}), f32[256,5120]{1,0:T(8,128)}) %all-reduce.4.cloned.1.call-update) | async-done | bytes 5242896 | tf_op jit(solution)/shard_map/psum | solution.py:22
  202.6 19.4 %fusion.1 = f32[256,3456]{0,1:T(8,128)} fusion(bf16[3456,5120]{1,0:T(8,128)(2,1)} %param.10, f32[256,5120]{1,0:T(8,128)} %all-reduce.4.cloned.1.call-done, bf16[256,5120]{1,0:T(8,128)(2,1)} %param.11), kind=kOutput, calls=%fused_computation.5 | convolution fusion | flops 9063628800 | bytes 46792704 | tf_op jit(solution)/shard_map/dot_general | solution.py:24
  222.0 5.3 %copy.40 = f32[256,16,216]{2,1,0:T(8,128)} copy(f32[256,16,216]{0,2,1:T(8,128)} %bitcast.63) | data formatting | bytes 7077888 | tf_op jit(solution)/shard_map/reshape | solution.py:27
  227.3 52.6 %all_to_all.71 = f32[256,16,216]{2,1,0:T(8,128)S(1)} all-to-all(f32[256,16,216]{2,1,0:T(8,128)} %copy.40), channel_id=1, replica_groups=mesh['dp'=4,'tensor'=8] {'tensor'}, dimensions={0} | all-to-all | bytes 7077888 | tf_op jit(solution)/shard_map/all_to_all | solution.py:28
  279.9 2.7 copy.41
  282.6 5.5 %copy.42 = f32[32,128,216]{1,2,0:T(8,128)} copy(f32[32,128,216]{2,1,0:T(8,128)} %bitcast.55) | data formatting | bytes 7077888 | tf_op jit(solution)/shard_map/all_to_all | solution.py:28
  288.1 6.4 %convolution_bitcast_fusion = f32[32,128,216]{1,2,0:T(8,128)} fusion(f32[32,128,216]{1,2,0:T(8,128)} %copy.42, f32[32,128,216]{1,2,0:T(8,128)} %get-tuple-element.15, f32[128,128]{1,0:T(8,128)S(1)} %copy-done.2), kind=kOutput, calls=%fused_computation.6 | convolution fusion | flops 1361608704 | bytes 10682368 | tf_op jit(solution)/shard_map/jl,tlk->tjk/dot_general | solution.py:30
  294.5 5.3 %copy.43 = f32[32,128,216]{2,0,1:T(8,128)} copy(f32[32,128,216]{1,2,0:T(8,128)} %convolution_bitcast_fusion) | data formatting | bytes 7077888 | tf_op jit(solution)/shard_map/jl,tlk->tjk/transpose | solution.py:30
  299.7 4.6 all-to-all-start.3
  304.5 10.7 %fusion.3 = f32[128,128]{1,0:T(8,128)} fusion(f32[32,128,216]{1,2,0:T(8,128)} %copy-done.1, f32[32,128,216]{1,2,0:T(8,128)} %copy.42, f32[32,128,216]{1,2,0:T(8,128)} %get-tuple-element.15), kind=kOutput, calls=%fused_computation.9 | convolution fusion | flops 1361608704 | bytes 10682368 | tf_op jit(solution)/shard_map/tjk,tlk->jl/dot_general | solution.py:31
  315.3 38.1 %all-to-all-done.3 = f32[32,128,216]{2,0,1:T(8,128)} async-done(((f32[32,128,216]{2,0,1:T(8,128)}), f32[32,128,216]{2,0,1:T(8,128)}, u32[]{:S(2)}, u32[]{:S(2)}) %all-to-all-start.3) | async-done | bytes 3538976 | tf_op jit(solution)/shard_map/all_to_all | solution.py:32
  353.4 6.5 %copy.45 = f32[8,32,16,216]{3,2,1,0:T(8,128)} copy(f32[8,32,16,216]{3,1,2,0:T(8,128)} %bitcast.17) | data formatting | bytes 7077888 | tf_op jit(solution)/shard_map/all_to_all | solution.py:32
  359.9 5.1 %copy.46 = f32[256,16,216]{0,2,1:T(8,128)} copy(f32[256,16,216]{2,1,0:T(8,128)} %bitcast.56) | data formatting | bytes 7077888 | tf_op jit(solution)/shard_map/all_to_all | solution.py:32
  365.0 4.6 convolution_bitcast_fusion.1
  369.6 7.1 %fusion.4 = f32[256,16,216]{0,2,1:T(8,128)} fusion(f32[256,16,216]{0,2,1:T(8,128)} %copy.46, f32[216,216]{1,0:T(8,128)S(1)} %copy-done), kind=kOutput, calls=%fused_computation.10 | convolution fusion | flops 2293235712 | bytes 7264512 | tf_op jit(solution)/shard_map/tjk,ik->tji/dot_general | solution.py:33
  376.7 5.2 %copy.49 = f32[256,3456]{1,0:T(8,128)} copy(f32[256,3456]{0,1:T(8,128)} %bitcast.59) | data formatting | bytes 7077888
  381.9 116.3 %all-reduce.6.cloned.1.call-done = (f32[216,216]{0,1:T(8,128)}, f32[128,128]{1,0:T(8,128)}) async-done(((f32[216,216]{0,1:T(8,128)}, f32[128,128]{1,0:T(8,128)}), (f32[216,216]{0,1:T(8,128)}, f32[128,128]{1,0:T(8,128)})) %all-reduce.6.cloned.1.call-update) | async-done | bytes 252176 | tf_op jit(solution)/shard_map/psum | solution.py:37
  (18 shorter events, 11.3 us)
Async XLA Ops:
  7.2 36.4 %copy-start = (f32[216,216]{1,0:T(8,128)S(1)}, f32[216,216]{1,0:T(8,128)}, u32[]{:S(2)}) copy-start(f32[216,216]{1,0:T(8,128)} %param.7) | copy-start | bytes 559876
  7.2 195.4 %all-reduce.4.cloned.1.call-start = ((), (), s32[]{:S(2)}) async-start(), calls=%async_computation.4 | async-start | bytes 10485760 | tf_op jit(solution)/shard_map/psum | solution.py:22
  43.5 2.2 copy-start.2
  43.5 2.2 copy-start.3
  45.7 4.7 copy-start.1
  299.7 53.7 %all-to-all-start.3 = ((f32[32,128,216]{2,0,1:T(8,128)}), f32[32,128,216]{2,0,1:T(8,128)}, u32[]{:S(2)}, u32[]{:S(2)}) async-start(f32[32,128,216]{2,0,1:T(8,128)} %copy.43), calls=%async_computation.3 | async-start | bytes 8388608 | tf_op jit(solution)/shard_map/all_to_all | solution.py:32
  304.3 193.9 %all-reduce.6.cloned.1.call-start = ((), (), s32[]{:S(2)}) async-start(), calls=%async_computation.5 | async-start | bytes 573440 | tf_op jit(solution)/shard_map/psum | solution.py:37
Sparse Core Ops, SparseCore 0:
  110.9 91.6 all-reduce.3
  369.7 128.4 all-reduce.5
where the time goes:
time: 510 us; the launch traced here: 508 us
  waiting for transfers between devices  246 us (48%)
  blocking collectives  113 us (22%)
  matrix products  72.9 us (14%)
  local copies, waits for them, and re-layouts  57 us (11%)
  between operations  14.1 us (3%)
    psum x1, waiting for transfers between devices, local(): left_sum, right_sum = lax.psum((left_part, right_part), ('dp', 'tensor'))  116 us
    psum x1, waiting for transfers between devices, local(): total = lax.psum(partial_out, 'tensor')  91.8 us
    all_to_all x1, blocking collectives, local(): lax.all_to_all(clipped_grad, 'tensor', split_axis=0, concat_axis=1, tiled...  52.6 us
    all_to_all x1, waiting for transfers between devices, local(): lax.all_to_all(mixed_grad, 'tensor', split_axis=1, concat_axis=0, tiled=T...  38.1 us
    all_to_all x1, blocking collectives, local(): lax.all_to_all(inputs, 'tensor', split_axis=0, concat_axis=1, tiled=True)  30.3 us
    all_to_all x1, blocking collectives, local(): lax.all_to_all(clipped, 'tensor', split_axis=1, concat_axis=0, tiled=True)  30.1 us
    dot_general x1, matrix products, local(): lax.dot_general(out_grad, weight_rows, (((1,), (1,)), ((), ())), preferre...  19.4 us
    dot_general x1, matrix products, local(): jnp.dot(clipped_back.reshape(tok_rows, -1), weight_rows, preferred_elemen...  18 us
  transfers between devices with their start and end apart: 3, of which 3 were waited for; matrix products, arithmetic and copies ran while one was open for 5% of the time, Pallas kernels for 0%

commit v1 on v0

--- a/solution.py
+++ b/solution.py
@@ -19,7 +19,7 @@
     partial_out = jnp.dot(
         clipped_back.reshape(tok_rows, -1), weight_rows, preferred_element_type=jnp.float32
     )
-    total = lax.psum(partial_out, "tensor")
+    total = jnp.sum(lax.all_gather(partial_out, "tensor"), axis=0)
     out_grad = (total - target.astype(jnp.float32)).astype(jnp.bfloat16)
     clipped_grad = lax.dot_general(
         out_grad, weight_rows, (((1,), (1,)), ((), ())), preferred_element_type=jnp.float32

time: 510 us -> 632 us (1.24)
  waiting for transfers between devices: 246 us -> 351 us
  other arithmetic: 0 us -> 18.1 us
    all_gather x0 -> x1, waiting for transfers between devices: none -> 196 us  [local(): total = jnp.sum(lax.all_gather(partial_out, 'tensor'), axis=0)]
    psum x1 -> x0, waiting for transfers between devices: 91.8 us -> none  [local(): total = lax.psum(partial_out, 'tensor')]
    reduce_sum x0 -> x1, other arithmetic: none -> 18.1 us  [local(): total = jnp.sum(lax.all_gather(partial_out, 'tensor'), axis=0)]
  transfers between devices with their start and end apart: 3 -> 3, of which waited for: 3 -> 3; matrix products, arithmetic and copies ran while one was open for 5% -> 4% of each run, Pallas kernels for 0% -> 0%
where the time goes in v1:
time: 632 us; the launch traced here: 631 us
  waiting for transfers between devices  351 us (56%)
  blocking collectives  113 us (18%)
  matrix products  72.9 us (12%)
  local copies, waits for them, and re-layouts  57 us (9%)
  other arithmetic  18.1 us (3%)
  between operations  14.1 us (2%)
    all_gather x1, waiting for transfers between devices, local(): total = jnp.sum(lax.all_gather(partial_out, 'tensor'), axis=0)  196 us
    psum x1, waiting for transfers between devices, local(): left_sum, right_sum = lax.psum((left_part, right_part), ('dp', 'tensor'))  116 us
    all_to_all x1, blocking collectives, local(): lax.all_to_all(clipped_grad, 'tensor', split_axis=0, concat_axis=1, tiled...  52.6 us
    all_to_all x1, waiting for transfers between devices, local(): lax.all_to_all(mixed_grad, 'tensor', split_axis=1, concat_axis=0, tiled=T...  38.3 us
    all_to_all x1, blocking collectives, local(): lax.all_to_all(inputs, 'tensor', split_axis=0, concat_axis=1, tiled=True)  30.3 us
    all_to_all x1, blocking collectives, local(): lax.all_to_all(clipped, 'tensor', split_axis=1, concat_axis=0, tiled=True)  30.1 us
    dot_general x1, matrix products, local(): lax.dot_general(out_grad, weight_rows, (((1,), (1,)), ((), ())), preferre...  19.4 us
    reduce_sum x1, other arithmetic, local(): total = jnp.sum(lax.all_gather(partial_out, 'tensor'), axis=0)  18.1 us
  transfers between devices with their start and end apart: 3, of which 3 were waited for; matrix products, arithmetic and copies ran while one was open for 4% of the time, Pallas kernels for 0%

profile of v1, /device:TPU:8, one launch (start us, length us, event | category | flops | bytes accessed | tf_op | source)
XLA Modules:
  0.0 630.9 jit_solution(16488020578709377023)
XLA Ops:
  9.9 3.0 copy.32
  12.9 30.3 %all_to_all.69 = bf16[256,16,216]{2,1,0:T(8,128)(2,1)S(1)} all-to-all(bf16[256,16,216]{2,1,0:T(8,128)(2,1)} %copy.32), channel_id=1, replica_groups=mesh['dp'=4,'tensor'=8] {'tensor'}, dimensions={0} | all-to-all | bytes 3538944 | tf_op jit(solution)/shard_map/all_to_all | solution.py:13
  45.7 4.7 multiply_convert_fusion
  50.4 4.5 copy.36
  54.9 30.1 %all_to_all.70 = bf16[32,128,216]{2,0,1:T(8,128)(2,1)S(1)} all-to-all(bf16[32,128,216]{2,0,1:T(8,128)(2,1)} %copy.36), channel_id=1, replica_groups=mesh['dp'=4,'tensor'=8] {'tensor'}, dimensions={1} | all-to-all | bytes 3538944 | tf_op jit(solution)/shard_map/all_to_all | solution.py:18
  87.6 5.1 reshape.21
  92.7 18.0 %fusion.12 = f32[256,5120]{1,0:T(8,128)} fusion(bf16[256,3456]{1,0:T(8,128)(2,1)} %reshape.21, bf16[3456,5120]{1,0:T(8,128)(2,1)} %param.10), kind=kOutput, calls=%fused_computation.18 | convolution fusion | flops 9059696640 | bytes 42401792 | tf_op jit(solution)/shard_map/dot_general | solution.py:19
  110.8 196.4 %all-gather.3.cloned.1.call-done = f32[2048,5120]{1,0:T(8,128)} async-done(((f32[256,5120]{1,0:T(8,128)}), f32[2048,5120]{1,0:T(8,128)}) %all-gather.3.cloned.1.call-update) | async-done | bytes 41943056 | tf_op jit(solution)/shard_map/all_gather | solution.py:22
  307.2 18.1 %reduce_sum.9 = f32[256,5120]{1,0:T(8,128)} reduce(f32[8,256,5120]{2,1,0:T(8,128)} %bitcast.55, f32[]{:T(128)} %constant.0.clone.1), dimensions={0}, to_apply=%region_0.0 | reduce | flops 9175040 | bytes 47185924 | tf_op jit(solution)/shard_map/reduce_sum | solution.py:22
  325.3 19.4 %fusion.1 = f32[256,3456]{0,1:T(8,128)} fusion(bf16[3456,5120]{1,0:T(8,128)(2,1)} %param.10, f32[256,5120]{1,0:T(8,128)} %reduce_sum.9, bf16[256,5120]{1,0:T(8,128)(2,1)} %param.11), kind=kOutput, calls=%fused_computation.5 | convolution fusion | flops 9063628800 | bytes 46792704 | tf_op jit(solution)/shard_map/dot_general | solution.py:24
  344.7 5.3 copy.40
  350.0 52.6 %all_to_all.71 = f32[256,16,216]{2,1,0:T(8,128)S(1)} all-to-all(f32[256,16,216]{2,1,0:T(8,128)} %copy.40), channel_id=1, replica_groups=mesh['dp'=4,'tensor'=8] {'tensor'}, dimensions={0} | all-to-all | bytes 7077888 | tf_op jit(solution)/shard_map/all_to_all | solution.py:28
  405.3 5.4 copy.42
  410.7 6.3 %convolution_bitcast_fusion = f32[32,128,216]{1,2,0:T(8,128)} fusion(f32[32,128,216]{1,2,0:T(8,128)} %copy.42, f32[32,128,216]{1,2,0:T(8,128)} %get-tuple-element.15, f32[128,128]{1,0:T(8,128)S(1)} %copy-done.2), kind=kOutput, calls=%fused_computation.6 | convolution fusion | flops 1361608704 | bytes 10682368 | tf_op jit(solution)/shard_map/jl,tlk->tjk/dot_general | solution.py:30
  417.1 5.3 copy.43
  422.3 4.6 all-to-all-start.3
  426.9 10.7 %fusion.3 = f32[128,128]{1,0:T(8,128)} fusion(f32[32,128,216]{1,2,0:T(8,128)} %copy-done.1, f32[32,128,216]{1,2,0:T(8,128)} %copy.42, f32[32,128,216]{1,2,0:T(8,128)} %get-tuple-element.15), kind=kOutput, calls=%fused_computation.9 | convolution fusion | flops 1361608704 | bytes 10682368 | tf_op jit(solution)/shard_map/tjk,tlk->jl/dot_general | solution.py:31
  437.7 38.3 %all-to-all-done.3 = f32[32,128,216]{2,0,1:T(8,128)} async-done(((f32[32,128,216]{2,0,1:T(8,128)}), f32[32,128,216]{2,0,1:T(8,128)}, u32[]{:S(2)}, u32[]{:S(2)}) %all-to-all-start.3) | async-done | bytes 3538976 | tf_op jit(solution)/shard_map/all_to_all | solution.py:32
  476.0 6.6 %copy.45 = f32[8,32,16,216]{3,2,1,0:T(8,128)} copy(f32[8,32,16,216]{3,1,2,0:T(8,128)} %bitcast.18) | data formatting | bytes 7077888 | tf_op jit(solution)/shard_map/all_to_all | solution.py:32
  482.6 5.1 copy.46
  487.7 4.6 convolution_bitcast_fusion.1
  492.3 7.1 %fusion.4 = f32[256,16,216]{0,2,1:T(8,128)} fusion(f32[256,16,216]{0,2,1:T(8,128)} %copy.46, f32[216,216]{1,0:T(8,128)S(1)} %copy-done), kind=kOutput, calls=%fused_computation.10 | convolution fusion | flops 2293235712 | bytes 7264512 | tf_op jit(solution)/shard_map/tjk,ik->tji/dot_general | solution.py:33
  499.4 5.2 copy.49
  504.5 116.3 %all-reduce.3.cloned.1.call-done = (f32[216,216]{0,1:T(8,128)}, f32[128,128]{1,0:T(8,128)}) async-done(((f32[216,216]{0,1:T(8,128)}, f32[128,128]{1,0:T(8,128)}), (f32[216,216]{0,1:T(8,128)}, f32[128,128]{1,0:T(8,128)})) %all-reduce.3.cloned.1.call-update) | async-done | bytes 252176 | tf_op jit(solution)/shard_map/psum | solution.py:37
  (19 shorter events, 13.6 us)
Async XLA Ops:
  7.2 36.4 %copy-start = (f32[216,216]{1,0:T(8,128)S(1)}, f32[216,216]{1,0:T(8,128)}, u32[]{:S(2)}) copy-start(f32[216,216]{1,0:T(8,128)} %param.7) | copy-start | bytes 559876
  7.2 300.0 %all-gather.3.cloned.1.call-start = ((), (), s32[]{:S(2)}) async-start(), calls=%async_computation.4 | async-start | bytes 47185920 | tf_op jit(solution)/shard_map/all_gather | solution.py:22
  43.5 2.2 copy-start.2
  43.5 2.2 copy-start.3
  45.7 4.7 copy-start.1
  422.3 53.7 %all-to-all-start.3 = ((f32[32,128,216]{2,0,1:T(8,128)}), f32[32,128,216]{2,0,1:T(8,128)}, u32[]{:S(2)}, u32[]{:S(2)}) async-start(f32[32,128,216]{2,0,1:T(8,128)} %copy.43), calls=%async_computation.3 | async-start | bytes 8388608 | tf_op jit(solution)/shard_map/all_to_all | solution.py:32
  426.9 194.0 %all-reduce.3.cloned.1.call-start = ((), (), s32[]{:S(2)}) async-start(), calls=%async_computation.5 | async-start | bytes 573440 | tf_op jit(solution)/shard_map/psum | solution.py:37
Sparse Core Ops, SparseCore 0:
  110.9 196.2 all-gather.2
  492.4 128.4 all-reduce.2
